TPU v7x, 128 devices: a whole 4x4x4 slice. The times are simulated.
128 devices in a mesh: dp: 8 (over z, core), sp: 16 (over y, x).
Axes of the slice: x: 4, y: 4, z: 4, core: 2. Of those that a mesh axis runs over, the one named last changes fastest.
Arguments:
- queries_in: bfloat16 [16, 16384, 16, 128], P('dp', 'sp'), may hold values from -6 to 6
- keys_in: bfloat16 [16, 16384, 16, 128], P('dp', 'sp'), may hold values from -6 to 6
- values_in: bfloat16 [16, 16384, 16, 128], P('dp', 'sp'), may hold values from -6 to 6
- out_weight: bfloat16 [2048, 2048], P('dp'), may hold values from -0.125 to 0.125
Outputs:
- block_out: bfloat16 [16, 16384, 2048], P('dp', 'sp')
All inputs are finite; a program needn't handle non-finite values.
Results may differ from a plain program's by a relative error of at most 0.006.
Values may be sent and summed in bfloat16 or wider, within the bound.
A program may use at most 320 MiB of HBM per device.

v0:
```python
import jax
import jax.numpy as jnp
from jax import lax
from jax.sharding import PartitionSpec as P


def together(arrays, axis):
    ends = [0]
    for a in arrays:
        ends.append(ends[-1] + a.size)
    so_far = lax.psum(jnp.concatenate([a.ravel() for a in arrays]), axis)
    return tuple((so_far[b:e].reshape(a.shape) for a, b, e in zip(arrays, ends, ends[1:])))


def feature_map(values):
    wide = values.astype(jnp.float32)
    return (wide * wide + 0.1).astype(jnp.bfloat16)


def finish_heads(read, count):
    result = read * count**0.5
    return result.astype(jnp.bfloat16)


def look_up(features, state, mass):
    top = jnp.einsum(
        "bthd,bhde->bthe", features, state.astype(jnp.bfloat16), preferred_element_type=jnp.float32
    )
    bottom = jnp.einsum("bthd,bhd->bth", features.astype(jnp.float32), mass)
    return top / (bottom + 0.001)[..., None]


def on_device(queries_in, keys_in, values_in, out_weight):
    query_feature, key_feature = (feature_map(queries_in), feature_map(keys_in))
    count = queries_in.shape[1] * lax.axis_size("sp")
    part_state = jnp.einsum(
        "bthd,bthe->bhde", key_feature, values_in, preferred_element_type=jnp.float32
    )
    part_mass = jnp.sum(key_feature.astype(jnp.float32), axis=1)
    state, mass = together((part_state, part_mass), "sp")
    read = look_up(query_feature, state / count, mass / count)
    mixed = finish_heads(read, count)
    mixed = mixed.reshape(mixed.shape[0], mixed.shape[1], -1)
    return jnp.einsum(
        "btw,wv->btv",
        mixed,
        lax.all_gather(out_weight, "dp", axis=0, tiled=True),
        preferred_element_type=jnp.float32,
    ).astype(jnp.bfloat16)


def solution(mesh):
    placed = (
        P("dp", "sp", None, None),
        P("dp", "sp", None, None),
        P("dp", "sp", None, None),
        P("dp", None),
    )
    return jax.shard_map(
        on_device, mesh=mesh, in_specs=placed, out_specs=P("dp", "sp", None), check_vma=False
    )
```

profile of v0, /device:TPU:0, one launch (start us, length us, event | category | flops | bytes accessed | tf_op | source)
XLA Modules:
  0.0 168.0 jit_solution(11725410266001708717)
XLA Ops:
  7.4 0.0 all-reduce.2.cloned.1.call-start
  7.4 9.5 %add_convert_fusion.1 = (bf16[2,1024,16,128]{3,2,1,0:T(8,128)(2,1)}, f32[2,16,128]{2,1,0:T(8,128)S(1)}) fusion(bf16[2,1024,16,128]{3,2,1,0:T(8,128)(2,1)} %param.5), kind=kLoop, calls=%fused_computation.5 | loop fusion | flops 25161728 | bytes 16793600 | tf_op jit(solution)/shard_map/convert_element_type | solution.py:17
  16.8 13.9 %fusion.4 = f32[2,16,128,128]{3,2,1,0:T(8,128)S(1)} fusion(bf16[2,1024,16,128]{3,2,1,0:T(8,128)(2,1)} %param.6, bf16[2,1024,16,128]{3,2,1,0:T(8,128)(2,1)} %get-tuple-element.5), kind=kOutput, calls=%fused_computation.8 | convolution fusion | flops 1073741824 | bytes 18874368 | tf_op jit(solution)/shard_map/bthd,bthe->bhde/dot_general | solution.py:36
  30.8 1.4 pad_maximum_fusion
  32.2 0.0 all-reduce.2.cloned.1.call-update
  32.2 0.2 all-gather.2.cloned.1.call-start
  32.5 0.3 all-gather.2.cloned.1.call-update
  32.8 8.9 %add_convert_fusion = bf16[2,1024,16,128]{3,2,1,0:T(8,128)(2,1)} fusion(bf16[2,1024,16,128]{3,2,1,0:T(8,128)(2,1)} %param.4), kind=kLoop, calls=%fused_computation.3 | loop fusion | flops 16777216 | bytes 16777216 | tf_op jit(solution)/shard_map/convert_element_type | solution.py:17
  41.7 12.6 %copy.16 = bf16[2,1024,16,128]{1,3,2,0:T(8,128)(2,1)} copy(bf16[2,1024,16,128]{3,2,1,0:T(8,128)(2,1)} %add_convert_fusion) | data formatting | bytes 16777216 | tf_op jit(solution)/shard_map/convert_element_type | solution.py:17
  54.3 71.2 %all-reduce.2.cloned.1.call-done = f32[528384]{0:T(1024)} async-done(((f32[528384]{0:T(1024)}), f32[528384]{0:T(1024)}) %all-reduce.2.cloned.1.call-update) | async-done | bytes 2113552 | tf_op jit(solution)/shard_map/psum | solution.py:11
  125.5 0.0 copy-start.1
  125.5 0.9 slice_multiply_fusion.1
  126.4 0.0 copy-start
  126.4 4.7 %fusion.12 = f32[2,16,1,1024]{3,2,1,0:T(1,128)S(1)} fusion(f32[2,16,128,1]{2,3,1,0:T(1,128)S(1)} %bitcast.33, bf16[2,1024,16,128]{1,3,2,0:T(8,128)(2,1)} %copy.16), kind=kOutput, calls=%fused_computation.18 | convolution fusion | flops 8388608 | bytes 8536064 | tf_op jit(solution)/shard_map/bthd,bhd->bth/dot_general | solution.py:29
  131.1 0.0 copy-done.1
  131.1 0.1 fusion.10
  131.3 1.0 copy-done
  132.3 4.5 %fusion.1 = bf16[2,1024,16,128]{1,3,2,0:T(8,128)(2,1)} fusion(f32[2,1024,16]{1,2,0:T(8,128)S(1)} %fusion.11, bf16[2,16,128,128]{3,2,1,0:T(8,128)(2,1)S(1)} %bitcast.32, bf16[2,1024,16,128]{1,3,2,0:T(8,128)(2,1)S(1)} %copy-done), kind=kOutput, calls=%fused_computation.2 | convolution fusion | flops 1086324736 | bytes 17956864 | tf_op jit(solution)/shard_map/bthd,bhde->bthe/dot_general | solution.py:26
  136.8 0.0 all-gather.2.cloned.1.call-done
  136.8 23.7 %fusion.7 = bf16[2,1024,2048]{2,1,0:T(8,128)(2,1)} fusion(bf16[2,1024,2048]{1,2,0:T(8,128)(2,1)} %bitcast.35, bf16[2048,2048]{1,0:T(8,128)(2,1)} %all-gather.2.cloned.1.call-done), kind=kOutput, calls=%fused_computation.11 | convolution fusion | flops 17184063488 | bytes 25165824 | tf_op jit(solution)/shard_map/btw,wv->btv/dot_general | solution.py:44
  (1 shorter events, 0.0 us)
Async XLA Ops:
  7.4 118.1 %all-reduce.2.cloned.1.call-start = ((), (), s32[]{:S(2)}) async-start(), calls=%async_computation | async-start | bytes 4227072 | tf_op jit(solution)/shard_map/psum | solution.py:11
  32.2 104.6 %all-gather.2.cloned.1.call-start = ((), (), s32[]{:S(2)}) async-start(), calls=%async_computation.1 | async-start | bytes 9437184 | tf_op jit(solution)/shard_map/all_gather | solution.py:47
  125.5 5.6 %copy-start.1 = (f32[528384]{0:T(1024)S(1)}, f32[528384]{0:T(1024)}, u32[]{:S(2)}) copy-start(f32[528384]{0:T(1024)} %all-reduce.2.cloned.1.call-done) | copy-start | bytes 6340612
  126.4 5.9 %copy-start = (bf16[2,1024,16,128]{1,3,2,0:T(8,128)(2,1)S(1)}, bf16[2,1024,16,128]{1,3,2,0:T(8,128)(2,1)}, u32[]{:S(2)}) copy-start(bf16[2,1024,16,128]{1,3,2,0:T(8,128)(2,1)} %copy.16) | copy-start | bytes 25165828
Sparse Core Ops, SparseCore 0:
  32.3 93.1 all-reduce.1
Sparse Core Ops, SparseCore 1:
  34.4 52.2 all-gather.1
where the time goes:
time: 168 us
  waiting for transfers between devices  71.5 us (43%)
  matrix products  46.9 us (28%)
  other arithmetic  20.9 us (12%)
  between operations  14.9 us (9%)
  local copies, waits for them, and re-layouts  13.6 us (8%)
    psum x1, waiting for transfers between devices, together(): so_far = lax.psum(jnp.concatenate([a.ravel() for a in arrays]), axis)  71.2 us
    dot_general x1, matrix products, on_device(): jnp.einsum('btw,wv->btv', mixed, lax.all_gather(out_weight, 'dp', axis=0,...  23.7 us
    convert_element_type x2, other arithmetic, feature_map(): return (wide * wide + 0.1).astype(jnp.bfloat16)  18.4 us
    dot_general x1, matrix products, on_device(): jnp.einsum('bthd,bthe->bhde', key_feature, values_in, preferred_element_t...  13.9 us
    convert_element_type x1, local copies, waits for them, and re-layouts, feature_map(): return (wide * wide + 0.1).astype(jnp.bfloat16)  12.6 us
    dot_general x1, matrix products, look_up(): bottom = jnp.einsum('bthd,bhd->bth', features.astype(jnp.float32), mass)  4.72 us
    dot_general x1, matrix products, look_up(): jnp.einsum('bthd,bhde->bthe', features, state.astype(jnp.bfloat16), prefe...  4.55 us
  transfers between devices with their start and end apart: 2, of which 1 were waited for; matrix products, arithmetic and copies ran while one was open for 19% of the time, Pallas kernels for 0%

commit v1 on v0

v1 whole, which is shorter than its diff:
```python
import functools

import jax
import jax.numpy as jnp
from jax import lax
from jax.experimental import pallas as pl
from jax.experimental.pallas import tpu as pltpu
from jax.sharding import PartitionSpec as P

MESH = pl.DeviceIdType.MESH
F32, BF16 = jnp.float32, jnp.bfloat16
B, T, H, D = 2, 1024, 16, 128
TB = 256
NC = T // TB
ROWS = 272
COUNT = 16384.0


def feature(x):
    wide = x.astype(F32)
    return (wide * wide + 0.1).astype(BF16)


def gather_kernel(
    k_hbm, v_hbm, w_hbm, w_out, st,
    kbuf, vbuf, wv, acc, macc, ps, r1, p2, r2, tmp,
    in_sem, loc_sem, out_sem,
    wz_s, wz_r, wp_s, wp_r, w1_s, w1_r, w2_s, w2_r, wd_s, wd_r,
    s1_s, s1_r, s2_s, s2_r, g1_s, g1_r, g2_s, g2_r,
):
    dp, sp = lax.axis_index("dp"), lax.axis_index("sp")
    z, c = dp // 2, dp % 2
    y, x = sp // 4, sp % 4
    a2, b2 = y * (1 - c) + x * c, x * (1 - c) + y * c

    def plane(dx, dy):
        return (dp, 4 * ((y + dy) % 4) + (x + dx) % 4)

    def along(dz):
        return (2 * ((z + dz) % 4) + c, sp)

    sibling = (2 * z + (1 - c), sp)

    def remote(src, dst, s, r, dev):
        return pltpu.make_async_remote_copy(
            src_ref=src, dst_ref=dst, send_sem=s, recv_sem=r, device_id=dev, device_id_type=MESH
        )

    def load(b, i):
        sl = pl.ds(i * TB, TB)
        n = b * NC + i
        return (
            pltpu.make_async_copy(k_hbm.at[b, sl], kbuf.at[b, sl], in_sem.at[0, n]),
            pltpu.make_async_copy(v_hbm.at[b, sl], vbuf.at[b, sl], in_sem.at[1, n]),
        )

    for b in range(B):
        for i in range(NC):
            for cp in load(b, i):
                cp.start()
    own = 2 * z + c
    keep = pltpu.make_async_copy(w_hbm, wv.at[own], loc_sem)
    keep.start()

    barrier = pltpu.get_barrier_semaphore()
    peers = [along(1), along(2), along(3), sibling]
    peers += [plane(o, 0) for o in (1, 2, 3)] + [plane(0, o) for o in (1, 2, 3)]
    for dev in peers:
        pl.semaphore_signal(barrier, inc=1, device_id=dev, device_id_type=MESH)
    acc[...] = jnp.zeros_like(acc)
    macc[...] = jnp.zeros_like(macc)
    tmp[...] = jnp.zeros_like(tmp)
    pl.semaphore_wait(barrier, len(peers))

    piece = pl.ds((4 * a2 + b2) * 16, 16)

    def far_send():
        return remote(w_hbm.at[piece], wv.at[own, piece], wp_s, wp_r, along(2))

    far = 2 * ((z + 2) % 4) + c

    def near(dz, i):
        k = 0 if dz == 1 else 1
        sl = pl.ds(i * 64, 64)
        return remote(w_hbm.at[sl], wv.at[own, sl], wz_s.at[k, i], wz_r.at[k, i], along(dz))

    def first(o):
        return remote(
            wv.at[far, piece], wv.at[far, piece], w1_s.at[o - 1], w1_r.at[o - 1],
            plane(o * (1 - c), o * c),
        )

    def second(o):
        sl = pl.ds(a2 * 64, 64)
        return remote(
            wv.at[far, sl], wv.at[far, sl], w2_s.at[o - 1], w2_r.at[o - 1],
            plane(o * c, o * (1 - c)),
        )

    def cross(src, dst, n):
        return remote(src, dst, wd_s.at[n], wd_r.at[n], sibling)

    def cross_own():
        return cross(w_hbm, wv.at[own], 0)

    def cross_near(dz, i):
        s = 2 * ((z + dz) % 4) + c
        sl = pl.ds(i * 64, 64)
        return cross(wv.at[s, sl], wv.at[s, sl], 1 + (0 if dz == 1 else 4) + i)

    def cross_far():
        return cross(wv.at[far], wv.at[far], 9)

    far_send().start()
    for i in range(4):
        near(1, i).start()
        near(3, i).start()
    cross_own().start()

    def coords(g):
        return (x, y) if g == 0 else (y, x)

    def ax1(g, o):
        return plane(o, 0) if g == 0 else plane(0, o)

    def ax2(g, o):
        return plane(0, o) if g == 0 else plane(o, 0)

    def rs1(b, g, o):
        a, _ = coords(g)
        n = b * 2 + g
        return remote(
            ps.at[b, g, (a + o) % 4], r1.at[b, g, o - 1], s1_s.at[n, o - 1], s1_r.at[n, o - 1], ax1(g, o)
        )

    def rs2(b, g, o):
        _, l = coords(g)
        n = b * 2 + g
        return remote(
            p2.at[b, g, (l + o) % 4], r2.at[b, g, o - 1], s2_s.at[n, o - 1], s2_r.at[n, o - 1], ax2(g, o)
        )

    def ag1(b, g, o):
        a, l = coords(g)
        n = b * 2 + g
        part = st.at[b, g, a, pl.ds(l * 64, 64)]
        return remote(part, part, g1_s.at[n, o - 1], g1_r.at[n, o - 1], ax2(g, o))

    def ag2(b, g, o):
        a, _ = coords(g)
        n = b * 2 + g
        part = st.at[b, g, a]
        return remote(part, part, g2_s.at[n, o - 1], g2_r.at[n, o - 1], ax1(g, o))

    def mass_block(total):
        hi = total.astype(BF16)
        lo = (total - hi.astype(F32)).astype(BF16)
        tmp[0:2, :] = hi.astype(F32)
        tmp[2:4, :] = lo.astype(F32)
        return tmp[...].astype(BF16)

    def start_rs1(b):
        mass = macc[b]
        for g in range(2):
            for j in range(4):
                h = g * 8 + 2 * j
                ps[b, g, j, 0:128, :] = acc[b, h].astype(BF16)
                ps[b, g, j, 128:256, :] = acc[b, h + 1].astype(BF16)
                ps[b, g, j, 256:272, :] = mass_block(mass[h : h + 2])
        for o in (2, 1, 3):
            for g in range(2):
                rs1(b, g, o).start()

    def start_rs2(b):
        for g in range(2):
            a, l = coords(g)
            for o in (1, 2, 3):
                rs1(b, g, o).wait_recv()
            h = g * 8 + 2 * a
            for half in range(2):
                rows = slice(half * 128, half * 128 + 128)
                total = acc[b, h + half]
                for s in range(3):
                    total = total + r1[b, g, s, rows, :].astype(F32)
                acc[b, h + half] = total
                low = total.astype(BF16)
                p2[b, g, 2 * half, 0:64, :] = low[0:64]
                p2[b, g, 2 * half + 1, 0:64, :] = low[64:128]
            blk = ps[b, g, a, 256:272, :].astype(F32)
            for s in range(3):
                blk = blk + r1[b, g, s, 256:272, :].astype(F32)
            out = mass_block(blk[0:2] + blk[2:4])
            for j in range(4):
                p2[b, g, j, 64:80, :] = out
            for o in (2, 1, 3):
                rs2(b, g, o).start()

    def start_ag1(b):
        for g in range(2):
            a, l = coords(g)
            for o in (1, 2, 3):
                rs2(b, g, o).wait_recv()
            h = g * 8 + 2 * a + l // 2
            total = acc[b, h, pl.ds((l % 2) * 64, 64), :]
            for s in range(3):
                total = total + r2[b, g, s, 0:64, :].astype(F32)
            st[b, g, a, pl.ds(l * 64, 64), :] = (total * (1.0 / COUNT)).astype(BF16)
            blk = p2[b, g, 0, 64:80, :].astype(F32)
            for s in range(3):
                blk = blk + r2[b, g, s, 64:80, :].astype(F32)
            st[b, g, a, 256:272, :] = mass_block((blk[0:2] + blk[2:4]) * (1.0 / COUNT))
            for o in (2, 1, 3):
                ag1(b, g, o).start()

    def start_ag2(b):
        for g in range(2):
            for o in (1, 2, 3):
                ag1(b, g, o).wait_recv()
            for o in (2, 1, 3):
                ag2(b, g, o).start()

    def end_ag2(b):
        for g in range(2):
            for o in (1, 2, 3):
                ag2(b, g, o).wait_recv()

    def start_first():
        remote(wv.at[far, piece], wv.at[far, piece], wp_s, wp_r, along(2)).wait_recv()
        for o in (2, 1, 3):
            first(o).start()

    def start_second():
        for o in (1, 2, 3):
            first(o).wait_recv()
        for o in (2, 1, 3):
            second(o).start()

    def near_arrived(dz, i):
        s = 2 * ((z + dz) % 4) + c
        sl = pl.ds(i * 64, 64)
        k = 1 if dz == 1 else 0
        remote(wv.at[s, sl], wv.at[s, sl], wz_s.at[k, i], wz_r.at[k, i], along(dz)).wait_recv()
        cross_near(dz, i).start()

    def chunk(n, _):
        b, i = n // NC, n % NC
        sl = pl.ds(pl.multiple_of(i * TB, TB), TB)
        for cp in load(b, i):
            cp.wait()
        kf = feature(kbuf[b, sl])
        macc[b] += jnp.sum(kf.astype(F32), axis=0)
        kt = jnp.swapaxes(kf, 0, 1)
        vt = jnp.swapaxes(vbuf[b, sl], 0, 1)
        for h in range(H):
            acc[b, h] += lax.dot_general(
                kt[h], vt[h], (((0,), (0,)), ((), ())), preferred_element_type=F32
            )

        @pl.when(n == 2)
        def _():
            start_first()

        @pl.when(n == 3)
        def _():
            start_rs1(0)

        @pl.when(n == 4)
        def _():
            start_second()

        @pl.when(n == 6)
        def _():
            start_rs2(0)

        @pl.when(n == 7)
        def _():
            start_rs1(1)

        return 0

    lax.fori_loop(0, B * NC, chunk, 0)
    start_ag1(0)
    for dz in (1, 3):
        near_arrived(dz, 0)
        near_arrived(dz, 1)
    start_ag2(0)
    start_rs2(1)
    for o in (1, 2, 3):
        second(o).wait_recv()
    cross_far().start()
    start_ag1(1)
    end_ag2(0)
    start_ag2(1)
    for i in (2, 3):
        for dz in (1, 3):
            near_arrived(dz, i)
    end_ag2(1)

    keep.wait()
    for n in range(10):
        if n == 0:
            s, sl = 2 * z + (1 - c), pl.ds(0, 256)
        elif n == 9:
            s, sl = 2 * ((z + 2) % 4) + (1 - c), pl.ds(0, 256)
        else:
            dz, i = (1, n - 1) if n < 5 else (3, n - 5)
            s, sl = 2 * ((z + dz) % 4) + (1 - c), pl.ds(i * 64, 64)
        cross(wv.at[s, sl], wv.at[s, sl], n).wait_recv()
    done = pltpu.make_async_copy(wv, w_out, out_sem)
    done.start()

    far_send().wait_send()
    for i in range(4):
        near(1, i).wait_send()
        near(3, i).wait_send()
        cross_near(1, i).wait_send()
        cross_near(3, i).wait_send()
    cross_own().wait_send()
    cross_far().wait_send()
    for o in (1, 2, 3):
        first(o).wait_send()
        second(o).wait_send()
        for b in range(B):
            for g in range(2):
                rs1(b, g, o).wait_send()
                rs2(b, g, o).wait_send()
                ag1(b, g, o).wait_send()
                ag2(b, g, o).wait_send()
    done.wait()


def gather(k, v, w):
    dma = pltpu.SemaphoreType.DMA
    return pl.pallas_call(
        gather_kernel,
        out_shape=(
            jax.ShapeDtypeStruct((8, 256, 2048), BF16),
            jax.ShapeDtypeStruct((B, 2, 4, ROWS, D), BF16),
        ),
        in_specs=[pl.BlockSpec(memory_space=pl.ANY)] * 3,
        out_specs=(pl.BlockSpec(memory_space=pl.ANY), pl.BlockSpec(memory_space=pltpu.VMEM)),
        scratch_shapes=[
            pltpu.VMEM((B, T, H, D), BF16),
            pltpu.VMEM((B, T, H, D), BF16),
            pltpu.VMEM((8, 256, 2048), BF16),
            pltpu.VMEM((B, H, D, D), F32),
            pltpu.VMEM((B, H, D), F32),
            pltpu.VMEM((B, 2, 4, ROWS, D), BF16),
            pltpu.VMEM((B, 2, 3, ROWS, D), BF16),
            pltpu.VMEM((B, 2, 4, 80, D), BF16),
            pltpu.VMEM((B, 2, 3, 80, D), BF16),
            pltpu.VMEM((16, D), F32),
            dma((2, B * NC)), dma, dma,
            dma((2, 4)), dma((2, 4)), dma, dma, dma((3,)), dma((3,)), dma((3,)), dma((3,)),
            dma((10,)), dma((10,)),
            dma((4, 3)), dma((4, 3)), dma((4, 3)), dma((4, 3)),
            dma((4, 3)), dma((4, 3)), dma((4, 3)), dma((4, 3)),
        ],
        compiler_params=pltpu.CompilerParams(
            collective_id=0, has_side_effects=True, vmem_limit_bytes=60 * 2**20
        ),
        name="gather",
    )(k, v, w)


def finish_kernel(q_ref, st_ref, w_ref, o_ref, rhs, mixed):
    b = pl.program_id(0)

    @pl.when(pl.program_id(1) == 0)
    def _():
        rhs[...] = jnp.zeros_like(rhs)
        for h in range(H):
            g, j, i = h // 8, (h % 8) // 2, h % 2
            rhs[h, 0:128, 0:128] = st_ref[b, g, j, i * 128 : (i + 1) * 128, :]
            blk = st_ref[b, g, j, 256:272, :].astype(F32)
            hi = jnp.broadcast_to(blk[i : i + 1], (128, 128))
            lo = jnp.broadcast_to(blk[2 + i : 3 + i], (128, 128))
            rhs[h, 0:128, 128:256] = hi.T.astype(BF16)
            rhs[h, 128:256, 128:256] = lo.T.astype(BF16)

    fq = jnp.swapaxes(feature(q_ref[0]), 0, 1)
    for h in range(H):
        r = jnp.dot(
            jnp.concatenate([fq[h], fq[h]], axis=1), rhs[h], preferred_element_type=F32
        )
        read = r[:, 0:128] / (r[:, 128:256] + 0.001)
        mixed[:, h * 128 : (h + 1) * 128] = (read * COUNT**0.5).astype(BF16)
    for n in range(4):
        cols = slice(n * 512, (n + 1) * 512)
        o_ref[0, :, cols] = jnp.dot(
            mixed[...], w_ref[:, cols], preferred_element_type=F32
        ).astype(BF16)


def finish(q, st, w):
    TM = 256
    return pl.pallas_call(
        finish_kernel,
        grid=(B, T // TM),
        in_specs=[
            pl.BlockSpec((1, TM, H, D), lambda b, i: (b, i, 0, 0)),
            pl.BlockSpec((B, 2, 4, ROWS, D), lambda b, i: (0, 0, 0, 0, 0)),
            pl.BlockSpec((2048, 2048), lambda b, i: (0, 0)),
        ],
        out_specs=pl.BlockSpec((1, TM, 2048), lambda b, i: (b, i, 0)),
        out_shape=jax.ShapeDtypeStruct((B, T, 2048), BF16),
        scratch_shapes=[pltpu.VMEM((H, 256, 256), BF16), pltpu.VMEM((TM, 2048), BF16)],
        compiler_params=pltpu.CompilerParams(vmem_limit_bytes=60 * 2**20),
        name="finish",
    )(q, st, w)


def on_device(queries_in, keys_in, values_in, out_weight):
    w, st = gather(keys_in, values_in, out_weight)
    return finish(queries_in, st, w.reshape(2048, 2048))


def solution(mesh):
    placed = (
        P("dp", "sp", None, None),
        P("dp", "sp", None, None),
        P("dp", "sp", None, None),
        P("dp", None),
    )
    return jax.shard_map(
        on_device, mesh=mesh, in_specs=placed, out_specs=P("dp", "sp", None), check_vma=False
    )
```

time: 168 us -> 83.4 us (0.50)
  Pallas kernels: 0 us -> 83.3 us
  waiting for transfers between devices: 71.5 us -> 0 us
  matrix products: 46.9 us -> 0 us
  other arithmetic: 20.9 us -> 0 us
  between operations: 14.9 us -> 0.01 us
  local copies, waits for them, and re-layouts: 13.6 us -> 0 us
    pallas_call x0 -> x2, Pallas kernels: none -> 83.3 us  [the longest x1 52.1 us: gather(): pl.pallas_call(gather_kernel, out_shape=(jax.ShapeDtypeStruct((8, 256, 20...]
    psum x1 -> x0, waiting for transfers between devices: 71.2 us -> none  [together(): so_far = lax.psum(jnp.concatenate([a.ravel() for a in arrays]), axis)]
    dot_general x4 -> x0, matrix products: 46.9 us -> none  [the longest x1 23.7 us: on_device(): jnp.einsum('btw,wv->btv', mixed, lax.all_gather(out_weight, 'dp', axis=0,...]
    convert_element_type x3 -> x0, other arithmetic: 18.5 us -> none  [the longest x2 18.4 us: feature_map(): return (wide * wide + 0.1).astype(jnp.bfloat16)]
    convert_element_type x1 -> x0, local copies, waits for them, and re-layouts: 12.6 us -> none  [feature_map(): return (wide * wide + 0.1).astype(jnp.bfloat16)]
  transfers between devices with their start and end apart: 2 -> 0, of which waited for: 1 -> 0; matrix products, arithmetic and copies ran while one was open for 19% -> 0% of each run, Pallas kernels for 0% -> 0%
where the time goes in v1:
time: 83.4 us; the launch traced here: 83.3 us
  Pallas kernels  83.3 us (100%)
    pallas_call x1, Pallas kernels, gather(): pl.pallas_call(gather_kernel, out_shape=(jax.ShapeDtypeStruct((8, 256, 20...  52.1 us
    pallas_call x1, Pallas kernels, finish(): pl.pallas_call(finish_kernel, grid=(B, T // TM), in_specs=[pl.BlockSpec((...  31.1 us

profile of v1, /device:TPU:0, one launch (start us, length us, event | category | flops | bytes accessed | tf_op | source)
XLA Modules:
  0.0 83.3 jit_solution(127739195727874605)
XLA Ops:
  0.0 52.1 %gather.1 = (bf16[8,256,2048]{2,1,0:T(8,128)(2,1)}, bf16[2,2,4,272,128]{4,3,2,1,0:T(8,128)(2,1)}) custom-call(bf16[2,1024,16,128]{3,2,1,0:T(8,128)(2,1)} %k_hbm.1, bf16[2,1024,16,128]{3,2,1,0:T(8,128)(2,1)} %v_hbm.1, bf16[256,2048]{1,0:T(8,128)(2,1)} %w_hbm.1), custom_call_target="tpu_custom_call" | custom-call | tf_op jit(solution)/shard_map/gather/pallas_call | solution.py:334
  52.1 31.1 %finish.1 = bf16[2,1024,2048]{2,1,0:T(8,128)(2,1)} custom-call(bf16[2,1024,16,128]{3,2,1,0:T(8,128)(2,1)} %q_ref.1, bf16[2,2,4,272,128]{4,3,2,1,0:T(8,128)(2,1)} %get-tuple-element.7.st_ref, bf16[2048,2048]{1,0:T(8,128)(2,1)} %bitcast.1), custom_call_target="tpu_custom_call" | custom-call | tf_op jit(solution)/shard_map/finish/pallas_call | solution.py:397

commit v2 on v1

v2 whole, which is shorter than its diff:
```python
import functools

import jax
import jax.numpy as jnp
from jax import lax
from jax.experimental import pallas as pl
from jax.experimental.pallas import tpu as pltpu
from jax.sharding import PartitionSpec as P

MESH = pl.DeviceIdType.MESH
F32, BF16 = jnp.float32, jnp.bfloat16
B, T, H, D = 2, 1024, 16, 128
TB = 512
PITCH = 20
STEP = 32
TM = 256
NC = T // TB
ROWS = 272
TN = 512
COUNT = 16384.0


def feature(x):
    wide = x.astype(F32)
    return (wide * wide + 0.1).astype(BF16)


def look_up_columns(st, rhs, cols_of):
    cols_of[...] = jnp.zeros_like(cols_of)
    for g in range(2):
        for j in range(4):
            h = g * 8 + 2 * j
            blk = st[g, j, 256:272, :].astype(F32)
            cols_of[h : h + 2, :] = blk[0:2]
            cols_of[16 + h : 18 + h, :] = blk[2:4]
    mass = cols_of[...].T
    for h in range(H):
        g, j, i = h // 8, (h % 8) // 2, h % 2
        rhs[h, 0:128, 0:128] = st[g, j, i * 128 : (i + 1) * 128, :]
        rhs[h, 128:256, 0:128] = jnp.zeros((128, 128), BF16)
        rhs[h, 0:128, 128:256] = jnp.broadcast_to(mass[:, h : h + 1], (128, 128)).astype(BF16)
        rhs[h, 128:256, 128:256] = jnp.broadcast_to(
            mass[:, 16 + h : 17 + h], (128, 128)
        ).astype(BF16)


def look_up(fq, rhs, mixed, lo, hi):
    def step(h, _):
        for t in range(T // TM):
            rows = slice(t * TM, (t + 1) * TM)
            f = fq[h, rows, :]
            r = jnp.dot(jnp.concatenate([f, f], axis=1), rhs[h], preferred_element_type=F32)
            read = r[:, 0:128] / (r[:, 128:256] + 0.001)
            mixed[rows, pl.ds(pl.multiple_of(h * D, D), D)] = (read * COUNT**0.5).astype(BF16)
        return 0

    lax.fori_loop(lo, hi, step, 0, unroll=4)


def gather_kernel(
    q_hbm, k_hbm, v_hbm, w_hbm, w_out, out0, fq1, st1,
    kbuf, vbuf, kf32, vf32, wv, acc, macc, ps, r1, xs, xr, st, tmp, fq, mixed, rhs, cols_of, obuf,
    in_sem, q_sem, loc_sem, out_sem, w_sem, m_sem,
    wz_s, wz_r, wp_s, wp_r, w1_s, w1_r, w2_s, w2_r, wd_s, wd_r,
    s1_s, s1_r, s2_s, s2_r, s3_s, s3_r,
):
    dp, sp = lax.axis_index("dp"), lax.axis_index("sp")
    z, c = dp // 2, dp % 2
    y, x = sp // 4, sp % 4
    a2, b2 = y * (1 - c) + x * c, x * (1 - c) + y * c

    def plane(dx, dy):
        return (dp, 4 * ((y + dy) % 4) + (x + dx) % 4)

    def along(dz):
        return (2 * ((z + dz) % 4) + c, sp)

    sibling = (2 * z + (1 - c), sp)

    def remote(src, dst, s, r, dev):
        return pltpu.make_async_remote_copy(
            src_ref=src, dst_ref=dst, send_sem=s, recv_sem=r, device_id=dev, device_id_type=MESH
        )

    def load(b, i):
        sl = pl.ds(i * TB, TB)
        n = b * NC + i
        return (
            pltpu.make_async_copy(k_hbm.at[b, sl], kbuf.at[b, sl], in_sem.at[0, n]),
            pltpu.make_async_copy(v_hbm.at[b, sl], vbuf.at[b, sl], in_sem.at[1, n]),
        )

    def load_q(b):
        return pltpu.make_async_copy(q_hbm.at[b], (kbuf, vbuf)[b].at[0], q_sem.at[b])

    for b in range(B):
        for i in range(NC):
            for cp in load(b, i):
                cp.start()
    own = 2 * z + c

    def shard(s):
        return pl.ds(pl.multiple_of(s * 256, 256), 256)

    keep = pltpu.make_async_copy(w_hbm, wv.at[shard(own)], loc_sem)
    keep.start()

    barrier = pltpu.get_barrier_semaphore()
    peers = [along(1), along(2), along(3), sibling]
    peers += [plane(o, 0) for o in (1, 2, 3)] + [plane(0, o) for o in (1, 2, 3)]
    for dev in peers:
        pl.semaphore_signal(barrier, inc=1, device_id=dev, device_id_type=MESH)
    acc[...] = jnp.zeros_like(acc)
    macc[...] = jnp.zeros_like(macc)
    tmp[...] = jnp.zeros_like(tmp)
    pl.semaphore_wait(barrier, len(peers))

    def far_rows(s, first, count):
        return pl.ds(pl.multiple_of(s * 256 + first * 16, 16), count * 16)

    far = 2 * ((z + 2) % 4) + c
    piece = 4 * a2 + b2

    def far_send():
        return remote(
            w_hbm.at[pl.ds(pl.multiple_of(piece * 16, 16), 16)], wv.at[far_rows(own, piece, 1)],
            wp_s, wp_r, along(2),
        )

    def near(dz, i):
        k = 0 if dz == 1 else 1
        cols = pl.ds(i * TN, TN)
        return remote(
            w_hbm.at[:, cols], wv.at[shard(own), cols], wz_s.at[k, i], wz_r.at[k, i], along(dz)
        )

    def first(o):
        part = wv.at[far_rows(far, piece, 1)]
        return remote(part, part, w1_s.at[o - 1], w1_r.at[o - 1], plane(o * (1 - c), o * c))

    def second(o):
        part = wv.at[far_rows(far, 4 * a2, 4)]
        return remote(part, part, w2_s.at[o - 1], w2_r.at[o - 1], plane(o * c, o * (1 - c)))

    def cross(src, dst, n):
        return remote(src, dst, wd_s.at[n], wd_r.at[n], sibling)

    def cross_own():
        return cross(w_hbm, wv.at[shard(own)], 0)

    def cross_near(dz, i):
        part = wv.at[shard(2 * ((z + dz) % 4) + c), pl.ds(i * TN, TN)]
        return cross(part, part, 1 + (0 if dz == 1 else 4) + i)

    def cross_far():
        part = wv.at[shard(far)]
        return cross(part, part, 9)

    far_send().start()
    for i in range(4):
        near(1, i).start()
        near(3, i).start()
    cross_own().start()

    def place(g):
        return x if g == 0 else y

    def ax1(g, o):
        return plane(o, 0) if g == 0 else plane(0, o)

    def ax2(g, o):
        return plane(0, o) if g == 0 else plane(o, 0)

    def scatter(b, g, o):
        n = b * 2 + g
        return remote(
            ps.at[b, g, (place(g) + o) % 4], r1.at[b, g, o - 1],
            s1_s.at[n, o - 1], s1_r.at[n, o - 1], ax1(g, o),
        )

    def exchange(b, g, o):
        n = b * 2 + g
        return remote(
            xs.at[b, g], xr.at[b, g, o - 1], s2_s.at[n, o - 1], s2_r.at[n, o - 1], ax2(g, o)
        )

    def spread(b, g, o):
        n = b * 2 + g
        part = st.at[b, g, place(g)]
        return remote(part, part, s3_s.at[n, o - 1], s3_r.at[n, o - 1], ax1(g, o))

    def mass_block(total):
        hi = total.astype(BF16)
        lo = (total - hi.astype(F32)).astype(BF16)
        tmp[0:2, :] = hi.astype(F32)
        tmp[2:4, :] = lo.astype(F32)
        return tmp[...].astype(BF16)

    def start_scatter(b):
        mass = macc[b]
        for g in range(2):
            for j in range(4):
                h = g * 8 + 2 * j
                ps[b, g, j, 0:128, :] = acc[b, h].astype(BF16)
                ps[b, g, j, 128:256, :] = acc[b, h + 1].astype(BF16)
                ps[b, g, j, 256:272, :] = mass_block(mass[h : h + 2])
        for o in (2, 1, 3):
            for g in range(2):
                scatter(b, g, o).start()

    def start_exchange(b):
        for g in range(2):
            a = place(g)
            for o in (1, 3, 2):
                scatter(b, g, o).wait_recv()
            h = g * 8 + 2 * a
            for i in range(2):
                rows = slice(i * 128, i * 128 + 128)
                total = acc[b, h + i]
                for s in range(3):
                    total = total + r1[b, g, s, rows, :].astype(F32)
                acc[b, h + i] = total
                xs[b, g, rows, :] = total.astype(BF16)
            blk = ps[b, g, a, 256:272, :].astype(F32)
            for s in range(3):
                blk = blk + r1[b, g, s, 256:272, :].astype(F32)
            xs[b, g, 256:272, :] = mass_block(blk[0:2] + blk[2:4])
            for o in (2, 1, 3):
                exchange(b, g, o).start()

    def start_spread(b):
        for g in range(2):
            a = place(g)
            for o in (1, 3, 2):
                exchange(b, g, o).wait_recv()
            h = g * 8 + 2 * a
            for i in range(2):
                rows = slice(i * 128, i * 128 + 128)
                total = acc[b, h + i]
                for s in range(3):
                    total = total + xr[b, g, s, rows, :].astype(F32)
                st[b, g, a, rows, :] = (total * (1.0 / COUNT)).astype(BF16)
            blk = xs[b, g, 256:272, :].astype(F32)
            for s in range(3):
                blk = blk + xr[b, g, s, 256:272, :].astype(F32)
            st[b, g, a, 256:272, :] = mass_block((blk[0:2] + blk[2:4]) * (1.0 / COUNT))
            for o in (2, 1, 3):
                spread(b, g, o).start()

    def end_spread(b):
        for g in range(2):
            for o in (1, 3, 2):
                spread(b, g, o).wait_recv()

    def start_first():
        part = wv.at[far_rows(far, piece, 1)]
        remote(part, part, wp_s, wp_r, along(2)).wait_recv()
        for o in (2, 1, 3):
            first(o).start()

    def start_second():
        for o in (1, 3, 2):
            first(o).wait_recv()
        for o in (2, 1, 3):
            second(o).start()

    def start_cross_far():
        for o in (1, 3, 2):
            second(o).wait_recv()
        cross_far().start()

    def start_cross_near(i):
        for dz in (1, 3):
            part = wv.at[shard(2 * ((z + dz) % 4) + c), pl.ds(i * TN, TN)]
            k = 1 if dz == 1 else 0
            remote(part, part, wz_s.at[k, i], wz_r.at[k, i], along(dz)).wait_recv()
            cross_near(dz, i).start()

    def wait_cross(n):
        if n == 0:
            part = wv.at[shard(2 * z + (1 - c))]
        elif n == 9:
            part = wv.at[shard(2 * ((z + 2) % 4) + (1 - c))]
        else:
            dz, i = (1, n - 1) if n < 5 else (3, n - 5)
            part = wv.at[shard(2 * ((z + dz) % 4) + (1 - c)), pl.ds(i * TN, TN)]
        cross(part, part, n).wait_recv()

    def chunk(n, _):
        b, i = n // NC, n % NC
        sl = pl.ds(pl.multiple_of(i * TB, TB), TB)
        for cp in load(b, i):
            cp.wait()

        def fill(j, mass):
            rows = []
            for t in range(STEP):
                at = i * TB + j * STEP + t
                f = feature(kbuf[b, at]).astype(F32)
                kf32[pl.ds((j * STEP + t) * PITCH, H), :] = f
                vf32[pl.ds((j * STEP + t) * PITCH, H), :] = vbuf[b, at].astype(F32)
                rows.append(f)
            while len(rows) > 1:
                rows = [p + q for p, q in zip(rows[::2], rows[1::2])]
            return mass + rows[0]

        macc[b] += lax.fori_loop(0, TB // STEP, fill, jnp.zeros((H, D), F32))
        for h in range(H):
            kh = kf32[pl.ds(h, TB, stride=PITCH), :].astype(BF16)
            vh = vf32[pl.ds(h, TB, stride=PITCH), :].astype(BF16)
            acc[b, h] += lax.dot_general(
                kh, vh, (((0,), (0,)), ((), ())), preferred_element_type=F32
            )

        @pl.when(n == 0)
        def _():
            start_first()

        @pl.when(n == NC - 1)
        def _():
            start_scatter(0)
            for b in range(B):
                load_q(b).start()

        return 0

    lax.fori_loop(0, B * NC, chunk, 0)
    start_second()
    start_exchange(0)
    start_scatter(1)
    start_cross_near(0)

    def turn(b):
        load_q(b).wait()

        q = (kbuf, vbuf)[b]

        def step(i, _):
            sl = pl.ds(pl.multiple_of(i * TM, TM), TM)
            fq[b, :, sl, :] = jnp.swapaxes(feature(q[0, sl]), 0, 1)
            return 0

        lax.fori_loop(0, T // TM, step, 0)

    turn(0)
    turn(1)
    put_fq = pltpu.make_async_copy(fq.at[1], fq1, m_sem.at[0])
    put_fq.start()
    start_spread(0)
    start_cross_far()
    start_exchange(1)
    start_cross_near(1)
    def put_out(n):
        return pltpu.make_async_copy(
            obuf.at[n % 2], out0.at[:, pl.ds(n * TN, TN)], out_sem.at[n]
        )

    def put_w(n):
        cols = pl.ds(n * TN, TN)
        return pltpu.make_async_copy(wv.at[:, cols], w_out.at[:, cols], w_sem.at[n])

    end_spread(0)
    look_up_columns(st.at[0], rhs, cols_of)
    look_up(fq.at[0], rhs, mixed, 0, H)
    start_cross_near(2)
    start_spread(1)
    keep.wait()
    wait_cross(0)
    wait_cross(9)
    for n in range(4):
        if n == 1:
            start_cross_near(3)
        if n == 3:
            end_spread(1)
            put_st = pltpu.make_async_copy(st.at[1], st1, m_sem.at[1])
            put_st.start()
        wait_cross(1 + n)
        wait_cross(5 + n)
        if n >= 2:
            put_out(n - 2).wait()
        cols = slice(n * TN, (n + 1) * TN)
        obuf[n % 2] = jnp.dot(mixed[...], wv[:, cols], preferred_element_type=F32).astype(BF16)
        put_out(n).start()
        put_w(n).start()

    far_send().wait_send()
    for i in range(4):
        near(1, i).wait_send()
        near(3, i).wait_send()
        cross_near(1, i).wait_send()
        cross_near(3, i).wait_send()
    cross_own().wait_send()
    cross_far().wait_send()
    for o in (1, 2, 3):
        first(o).wait_send()
        second(o).wait_send()
        for b in range(B):
            for g in range(2):
                scatter(b, g, o).wait_send()
                exchange(b, g, o).wait_send()
                spread(b, g, o).wait_send()
    for n in range(4):
        put_w(n).wait()
    put_out(2).wait()
    put_out(3).wait()
    put_fq.wait()
    put_st.wait()


def gather(q, k, v, w):
    dma = pltpu.SemaphoreType.DMA
    hbm = pl.BlockSpec(memory_space=pl.ANY)
    return pl.pallas_call(
        gather_kernel,
        out_shape=(
            jax.ShapeDtypeStruct((2048, 2048), BF16),
            jax.ShapeDtypeStruct((T, 2048), BF16),
            jax.ShapeDtypeStruct((H, T, D), BF16),
            jax.ShapeDtypeStruct((2, 4, ROWS, D), BF16),
        ),
        in_specs=[hbm] * 4,
        out_specs=(hbm,) * 4,
        scratch_shapes=[
            pltpu.VMEM((B, T, H, D), BF16),
            pltpu.VMEM((B, T, H, D), BF16),
            pltpu.VMEM((TB * PITCH, D), F32),
            pltpu.VMEM((TB * PITCH, D), F32),
            pltpu.VMEM((2048, 2048), BF16),
            pltpu.VMEM((B, H, D, D), F32),
            pltpu.VMEM((B, H, D), F32),
            pltpu.VMEM((B, 2, 4, ROWS, D), BF16),
            pltpu.VMEM((B, 2, 3, ROWS, D), BF16),
            pltpu.VMEM((B, 2, ROWS, D), BF16),
            pltpu.VMEM((B, 2, 3, ROWS, D), BF16),
            pltpu.VMEM((B, 2, 4, ROWS, D), BF16),
            pltpu.VMEM((16, D), F32),
            pltpu.VMEM((B, H, T, D), BF16),
            pltpu.VMEM((T, 2048), BF16),
            pltpu.VMEM((H, 256, 256), BF16),
            pltpu.VMEM((D, D), F32),
            pltpu.VMEM((2, T, TN), BF16),
            dma((2, B * NC)), dma((B,)), dma, dma((4,)), dma((4,)), dma((2,)),
            dma((2, 4)), dma((2, 4)), dma, dma, dma((3,)), dma((3,)), dma((3,)), dma((3,)),
            dma((10,)), dma((10,)),
            dma((4, 3)), dma((4, 3)), dma((4, 3)), dma((4, 3)), dma((4, 3)), dma((4, 3)),
        ],
        compiler_params=pltpu.CompilerParams(
            collective_id=0, has_side_effects=True, vmem_limit_bytes=63 * 2**20
        ),
        name="gather",
    )(q, k, v, w)


def finish_kernel(
    fq_hbm, st_ref, w_hbm, first_hbm, o_hbm,
    fq, rhs, cols_of, mixed, wbuf, fbuf, obuf, q_sem, w_sem, f_sem, o_sem,
):
    def get_q(n):
        hs = pl.ds(n * 4, 4)
        return pltpu.make_async_copy(fq_hbm.at[hs], fq.at[hs], q_sem.at[n])

    def get_w(n):
        cols = pl.ds(n * TN, TN)
        return pltpu.make_async_copy(w_hbm.at[:, cols], wbuf.at[:, cols], w_sem.at[n])

    def put(n):
        return pltpu.make_async_copy(
            obuf.at[n % 2], o_hbm.at[1, :, pl.ds(n * TN, TN)], o_sem.at[n]
        )

    for n in range(4):
        get_q(n).start()
    for n in range(4):
        get_w(n).start()
    get_first = pltpu.make_async_copy(first_hbm, fbuf, f_sem.at[0])
    get_first.start()
    put_first = pltpu.make_async_copy(fbuf, o_hbm.at[0], f_sem.at[1])
    look_up_columns(st_ref, rhs, cols_of)
    for n in range(4):
        get_q(n).wait()
    look_up(fq, rhs, mixed, 0, H)
    for n in range(4):
        get_w(n).wait()
        if n == 0:
            get_first.wait()
            put_first.start()
        if n >= 2:
            put(n - 2).wait()
        cols = slice(n * TN, (n + 1) * TN)
        obuf[n % 2] = jnp.dot(mixed[...], wbuf[:, cols], preferred_element_type=F32).astype(BF16)
        put(n).start()
    put_first.wait()
    put(2).wait()
    put(3).wait()


def finish(fq1, st1, w, out0):
    dma = pltpu.SemaphoreType.DMA
    hbm = pl.BlockSpec(memory_space=pl.ANY)
    return pl.pallas_call(
        finish_kernel,
        in_specs=[hbm, pl.BlockSpec(memory_space=pltpu.VMEM), hbm, hbm],
        out_specs=hbm,
        out_shape=jax.ShapeDtypeStruct((B, T, 2048), BF16),
        scratch_shapes=[
            pltpu.VMEM((H, T, D), BF16),
            pltpu.VMEM((H, 256, 256), BF16),
            pltpu.VMEM((D, D), F32),
            pltpu.VMEM((T, 2048), BF16),
            pltpu.VMEM((2048, 2048), BF16),
            pltpu.VMEM((T, 2048), BF16),
            pltpu.VMEM((2, T, TN), BF16),
            dma((4,)), dma((4,)), dma((2,)), dma((4,)),
        ],
        compiler_params=pltpu.CompilerParams(vmem_limit_bytes=60 * 2**20),
        name="finish",
    )(fq1, st1, w, out0)


def on_device(queries_in, keys_in, values_in, out_weight):
    w, out0, fq1, st1 = gather(queries_in, keys_in, values_in, out_weight)
    return finish(fq1, st1, w, out0)


def solution(mesh):
    placed = (
        P("dp", "sp", None, None),
        P("dp", "sp", None, None),
        P("dp", "sp", None, None),
        P("dp", None),
    )
    return jax.shard_map(
        on_device, mesh=mesh, in_specs=placed, out_specs=P("dp", "sp", None), check_vma=False
    )
```

time: 83.4 us -> 69.8 us (0.84)
  Pallas kernels: 83.3 us -> 69.5 us
    pallas_call x2, Pallas kernels: 83.3 us -> 69.5 us  [the longest x1 50.8 us: gather(): pl.pallas_call(gather_kernel, out_shape=(jax.ShapeDtypeStruct((2048, 2048...]
where the time goes in v2:
time: 69.8 us; the launch traced here: 69.6 us
  Pallas kernels  69.5 us (100%)
    pallas_call x1, Pallas kernels, gather(): pl.pallas_call(gather_kernel, out_shape=(jax.ShapeDtypeStruct((2048, 2048...  50.8 us
    pallas_call x1, Pallas kernels, finish(): pl.pallas_call(finish_kernel, in_specs=[hbm, pl.BlockSpec(memory_space=pl...  18.7 us

profile of v2, /device:TPU:0, one launch (start us, length us, event | category | flops | bytes accessed | tf_op | source)
XLA Modules:
  0.0 69.6 jit_solution(14260419896281405285)
XLA Ops:
  0.0 50.8 %gather.1 = (bf16[2048,2048]{1,0:T(8,128)(2,1)}, bf16[1024,2048]{1,0:T(8,128)(2,1)}, bf16[16,1024,128]{2,1,0:T(8,128)(2,1)}, bf16[2,4,272,128]{3,2,1,0:T(8,128)(2,1)}) custom-call(bf16[2,1024,16,128]{3,2,1,0:T(8,128)(2,1)} %q_hbm.1, bf16[2,1024,16,128]{3,2,1,0:T(8,128)(2,1)} %k_hbm.1, bf16[2,1024,16,128]{3,2,1,0:T(8,128)(2,1)} %v_hbm.1, bf16[256,2048]{1,0:T(8,128)(2,1)} %w_hbm.1), custom_call_target="tpu_custom_call" | custom-call | tf_op jit(solution)/shard_map/gather/pallas_call | solution.py:413
  50.8 18.7 %finish.1 = bf16[2,1024,2048]{2,1,0:T(8,128)(2,1)} custom-call(bf16[16,1024,128]{2,1,0:T(8,128)(2,1)} %get-tuple-element.9.fq_hbm, bf16[2,4,272,128]{3,2,1,0:T(8,128)(2,1)} %get-tuple-element.10.st_ref, bf16[2048,2048]{1,0:T(8,128)(2,1)} %get-tuple-element.11.w_hbm, bf16[1024,2048]{1,0:T(8,128)(2,1)} %get-tuple-element.12.first_hbm), custom_call_target="tpu_custom_call" | custom-call | tf_op jit(solution)/shard_map/finish/pallas_call | solution.py:500

commit v3 on v2

--- a/solution.py
+++ b/solution.py
@@ -11,12 +11,14 @@
 F32, BF16 = jnp.float32, jnp.bfloat16
 B, T, H, D = 2, 1024, 16, 128
 TB = 512
+HB = 256
 PITCH = 20
 STEP = 32
 TM = 256
 NC = T // TB
 ROWS = 272
 TN = 512
+CN = 1024
 COUNT = 16384.0
 
 
@@ -25,36 +27,27 @@
     return (wide * wide + 0.1).astype(BF16)
 
 
-def look_up_columns(st, rhs, cols_of):
-    cols_of[...] = jnp.zeros_like(cols_of)
+def look_up(fq, st, rhs, cols_of, mixed, owners):
+    heads = []
     for g in range(2):
-        for j in range(4):
-            h = g * 8 + 2 * j
-            blk = st[g, j, 256:272, :].astype(F32)
-            cols_of[h : h + 2, :] = blk[0:2]
-            cols_of[16 + h : 18 + h, :] = blk[2:4]
+        j = owners[g]
+        blk = st[g, j, 256:272, :].astype(F32)
+        cols_of[4 * g : 4 * g + 4, :] = blk[0:4]
+        heads += [(g, j, 0), (g, j, 1)]
     mass = cols_of[...].T
-    for h in range(H):
-        g, j, i = h // 8, (h % 8) // 2, h % 2
-        rhs[h, 0:128, 0:128] = st[g, j, i * 128 : (i + 1) * 128, :]
-        rhs[h, 128:256, 0:128] = jnp.zeros((128, 128), BF16)
-        rhs[h, 0:128, 128:256] = jnp.broadcast_to(mass[:, h : h + 1], (128, 128)).astype(BF16)
-        rhs[h, 128:256, 128:256] = jnp.broadcast_to(
-            mass[:, 16 + h : 17 + h], (128, 128)
-        ).astype(BF16)
-
-
-def look_up(fq, rhs, mixed, lo, hi):
-    def step(h, _):
+    for n, (g, j, i) in enumerate(heads):
+        hi, lo = 4 * g + i, 4 * g + 2 + i
+        rhs[n, 0:128, 0:128] = st[g, j, i * 128 : (i + 1) * 128, :]
+        rhs[n, 0:128, 128:256] = jnp.broadcast_to(mass[:, hi : hi + 1], (128, 128)).astype(BF16)
+        rhs[n, 128:256, 128:256] = jnp.broadcast_to(mass[:, lo : lo + 1], (128, 128)).astype(BF16)
+    for n, (g, j, i) in enumerate(heads):
+        h = g * 8 + 2 * j + i
         for t in range(T // TM):
             rows = slice(t * TM, (t + 1) * TM)
             f = fq[h, rows, :]
-            r = jnp.dot(jnp.concatenate([f, f], axis=1), rhs[h], preferred_element_type=F32)
+            r = jnp.dot(jnp.concatenate([f, f], axis=1), rhs[n], preferred_element_type=F32)
             read = r[:, 0:128] / (r[:, 128:256] + 0.001)
             mixed[rows, pl.ds(pl.multiple_of(h * D, D), D)] = (read * COUNT**0.5).astype(BF16)
-        return 0
-
-    lax.fori_loop(lo, hi, step, 0, unroll=4)
 
 
 def gather_kernel(
@@ -82,28 +75,29 @@
             src_ref=src, dst_ref=dst, send_sem=s, recv_sem=r, device_id=dev, device_id_type=MESH
         )
 
-    def load(b, i):
-        sl = pl.ds(i * TB, TB)
-        n = b * NC + i
+    def load(b, i, half):
+        sl = pl.ds(i * TB + half * HB, HB)
+        n = 2 * (b * NC + i) + half
         return (
             pltpu.make_async_copy(k_hbm.at[b, sl], kbuf.at[b, sl], in_sem.at[0, n]),
             pltpu.make_async_copy(v_hbm.at[b, sl], vbuf.at[b, sl], in_sem.at[1, n]),
         )
 
+    def start_load(b, i):
+        for half in range(2):
+            for cp in load(b, i, half):
+                cp.start()
+
     def load_q(b):
         return pltpu.make_async_copy(q_hbm.at[b], (kbuf, vbuf)[b].at[0], q_sem.at[b])
 
-    for b in range(B):
-        for i in range(NC):
-            for cp in load(b, i):
-                cp.start()
+    start_load(0, 0)
     own = 2 * z + c
 
     def shard(s):
         return pl.ds(pl.multiple_of(s * 256, 256), 256)
 
     keep = pltpu.make_async_copy(w_hbm, wv.at[shard(own)], loc_sem)
-    keep.start()
 
     barrier = pltpu.get_barrier_semaphore()
     peers = [along(1), along(2), along(3), sibling]
@@ -113,6 +107,8 @@
     acc[...] = jnp.zeros_like(acc)
     macc[...] = jnp.zeros_like(macc)
     tmp[...] = jnp.zeros_like(tmp)
+    cols_of[...] = jnp.zeros_like(cols_of)
+    rhs[...] = jnp.zeros_like(rhs)
     pl.semaphore_wait(barrier, len(peers))
 
     def far_rows(s, first, count):
@@ -138,9 +134,11 @@
         part = wv.at[far_rows(far, piece, 1)]
         return remote(part, part, w1_s.at[o - 1], w1_r.at[o - 1], plane(o * (1 - c), o * c))
 
-    def second(o):
-        part = wv.at[far_rows(far, 4 * a2, 4)]
-        return remote(part, part, w2_s.at[o - 1], w2_r.at[o - 1], plane(o * c, o * (1 - c)))
+    def second(o, i):
+        part = wv.at[far_rows(far, 4 * a2, 4), pl.ds(i * CN, CN)]
+        return remote(
+            part, part, w2_s.at[i, o - 1], w2_r.at[i, o - 1], plane(o * c, o * (1 - c))
+        )
 
     def cross(src, dst, n):
         return remote(src, dst, wd_s.at[n], wd_r.at[n], sibling)
@@ -152,15 +150,16 @@
         part = wv.at[shard(2 * ((z + dz) % 4) + c), pl.ds(i * TN, TN)]
         return cross(part, part, 1 + (0 if dz == 1 else 4) + i)
 
-    def cross_far():
-        part = wv.at[shard(far)]
-        return cross(part, part, 9)
+    def cross_far(i):
+        part = wv.at[shard(far), pl.ds(i * CN, CN)]
+        return cross(part, part, 9 + i)
 
     far_send().start()
     for i in range(4):
         near(1, i).start()
         near(3, i).start()
     cross_own().start()
+    start_load(0, 1)
 
     def place(g):
         return x if g == 0 else y
@@ -258,16 +257,17 @@
         for o in (2, 1, 3):
             first(o).start()
 
-    def start_second():
+    def start_second(i):
+        if i == 0:
+            for o in (1, 3, 2):
+                first(o).wait_recv()
+        for o in (2, 1, 3):
+            second(o, i).start()
+
+    def start_cross_far(i):
         for o in (1, 3, 2):
-            first(o).wait_recv()
-        for o in (2, 1, 3):
-            second(o).start()
-
-    def start_cross_far():
-        for o in (1, 3, 2):
-            second(o).wait_recv()
-        cross_far().start()
+            second(o, i).wait_recv()
+        cross_far(i).start()
 
     def start_cross_near(i):
         for dz in (1, 3):
@@ -279,8 +279,8 @@
     def wait_cross(n):
         if n == 0:
             part = wv.at[shard(2 * z + (1 - c))]
-        elif n == 9:
-            part = wv.at[shard(2 * ((z + 2) % 4) + (1 - c))]
+        elif n >= 9:
+            part = wv.at[shard(2 * ((z + 2) % 4) + (1 - c)), pl.ds((n - 9) * CN, CN)]
         else:
             dz, i = (1, n - 1) if n < 5 else (3, n - 5)
             part = wv.at[shard(2 * ((z + dz) % 4) + (1 - c)), pl.ds(i * TN, TN)]
@@ -288,9 +288,9 @@
 
     def chunk(n, _):
         b, i = n // NC, n % NC
-        sl = pl.ds(pl.multiple_of(i * TB, TB), TB)
-        for cp in load(b, i):
-            cp.wait()
+        @pl.when(n + 2 < B * NC)
+        def _():
+            start_load((n + 2) // NC, (n + 2) % NC)
 
         def fill(j, mass):
             rows = []
@@ -304,7 +304,12 @@
                 rows = [p + q for p, q in zip(rows[::2], rows[1::2])]
             return mass + rows[0]
 
-        macc[b] += lax.fori_loop(0, TB // STEP, fill, jnp.zeros((H, D), F32))
+        mass = jnp.zeros((H, D), F32)
+        for half in range(2):
+            for cp in load(b, i, half):
+                cp.wait()
+            mass = lax.fori_loop(half * (HB // STEP), (half + 1) * (HB // STEP), fill, mass)
+        macc[b] += mass
         for h in range(H):
             kh = kf32[pl.ds(h, TB, stride=PITCH), :].astype(BF16)
             vh = vf32[pl.ds(h, TB, stride=PITCH), :].astype(BF16)
@@ -319,14 +324,15 @@
         @pl.when(n == NC - 1)
         def _():
             start_scatter(0)
+            keep.start()
             for b in range(B):
                 load_q(b).start()
 
         return 0
 
     lax.fori_loop(0, B * NC, chunk, 0)
-    start_second()
     start_exchange(0)
+    start_second(0)
     start_scatter(1)
     start_cross_near(0)
 
@@ -347,41 +353,46 @@
     put_fq = pltpu.make_async_copy(fq.at[1], fq1, m_sem.at[0])
     put_fq.start()
     start_spread(0)
-    start_cross_far()
-    start_exchange(1)
-    start_cross_near(1)
+    start_second(1)
     def put_out(n):
-        return pltpu.make_async_copy(
-            obuf.at[n % 2], out0.at[:, pl.ds(n * TN, TN)], out_sem.at[n]
-        )
+        cols = pl.ds(n * TN, TN)
+        return pltpu.make_async_copy(obuf.at[:, cols], out0.at[:, cols], out_sem.at[n])
 
     def put_w(n):
         cols = pl.ds(n * TN, TN)
         return pltpu.make_async_copy(wv.at[:, cols], w_out.at[:, cols], w_sem.at[n])
 
-    end_spread(0)
-    look_up_columns(st.at[0], rhs, cols_of)
-    look_up(fq.at[0], rhs, mixed, 0, H)
+    for o in (0, 1, 3, 2):
+        if o == 1:
+            start_cross_near(1)
+            start_exchange(1)
+            start_cross_far(0)
+        if o:
+            for g in range(2):
+                spread(0, g, o).wait_recv()
+        owners = [(place(g) + 4 - o) % 4 for g in range(2)]
+        look_up(fq.at[0], st.at[0], rhs, cols_of, mixed, owners)
+    start_spread(1)
     start_cross_near(2)
-    start_spread(1)
+    start_cross_far(1)
     keep.wait()
     wait_cross(0)
     wait_cross(9)
     for n in range(4):
         if n == 1:
             start_cross_near(3)
+        if n == 2:
+            wait_cross(10)
         if n == 3:
             end_spread(1)
             put_st = pltpu.make_async_copy(st.at[1], st1, m_sem.at[1])
             put_st.start()
         wait_cross(1 + n)
         wait_cross(5 + n)
-        if n >= 2:
-            put_out(n - 2).wait()
         cols = slice(n * TN, (n + 1) * TN)
-        obuf[n % 2] = jnp.dot(mixed[...], wv[:, cols], preferred_element_type=F32).astype(BF16)
+        put_w(n).start()
+        obuf[:, cols] = jnp.dot(mixed[...], wv[:, cols], preferred_element_type=F32).astype(BF16)
         put_out(n).start()
-        put_w(n).start()
 
     far_send().wait_send()
     for i in range(4):
@@ -390,10 +401,12 @@
         cross_near(1, i).wait_send()
         cross_near(3, i).wait_send()
     cross_own().wait_send()
-    cross_far().wait_send()
+    for i in range(2):
+        cross_far(i).wait_send()
     for o in (1, 2, 3):
         first(o).wait_send()
-        second(o).wait_send()
+        for i in range(2):
+            second(o, i).wait_send()
         for b in range(B):
             for g in range(2):
                 scatter(b, g, o).wait_send()
@@ -401,8 +414,7 @@
                 spread(b, g, o).wait_send()
     for n in range(4):
         put_w(n).wait()
-    put_out(2).wait()
-    put_out(3).wait()
+        put_out(n).wait()
     put_fq.wait()
     put_st.wait()
 
@@ -436,12 +448,12 @@
             pltpu.VMEM((16, D), F32),
             pltpu.VMEM((B, H, T, D), BF16),
             pltpu.VMEM((T, 2048), BF16),
-            pltpu.VMEM((H, 256, 256), BF16),
+            pltpu.VMEM((4, 256, 256), BF16),
             pltpu.VMEM((D, D), F32),
-            pltpu.VMEM((2, T, TN), BF16),
-            dma((2, B * NC)), dma((B,)), dma, dma((4,)), dma((4,)), dma((2,)),
-            dma((2, 4)), dma((2, 4)), dma, dma, dma((3,)), dma((3,)), dma((3,)), dma((3,)),
-            dma((10,)), dma((10,)),
+            pltpu.VMEM((T, 2048), BF16),
+            dma((2, 2 * B * NC)), dma((B,)), dma, dma((4,)), dma((4,)), dma((2,)),
+            dma((2, 4)), dma((2, 4)), dma, dma, dma((3,)), dma((3,)), dma((2, 3)), dma((2, 3)),
+            dma((11,)), dma((11,)),
             dma((4, 3)), dma((4, 3)), dma((4, 3)), dma((4, 3)), dma((4, 3)), dma((4, 3)),
         ],
         compiler_params=pltpu.CompilerParams(
@@ -452,46 +464,58 @@
 
 
 def finish_kernel(
-    fq_hbm, st_ref, w_hbm, first_hbm, o_hbm,
-    fq, rhs, cols_of, mixed, wbuf, fbuf, obuf, q_sem, w_sem, f_sem, o_sem,
+    fq_hbm, st_hbm, w_hbm, first_hbm, o_hbm,
+    fq, st, rhs, cols_of, mixed, wbuf, fbuf, obuf, q_sem, s_sem, w_sem, f_sem, o_sem,
 ):
-    def get_q(n):
-        hs = pl.ds(n * 4, 4)
-        return pltpu.make_async_copy(fq_hbm.at[hs], fq.at[hs], q_sem.at[n])
+    def get_q(n, g):
+        hs = pl.ds(g * 8 + 2 * n, 2)
+        return pltpu.make_async_copy(fq_hbm.at[hs], fq.at[hs], q_sem.at[n, g])
 
     def get_w(n):
         cols = pl.ds(n * TN, TN)
         return pltpu.make_async_copy(w_hbm.at[:, cols], wbuf.at[:, cols], w_sem.at[n])
 
-    def put(n):
-        return pltpu.make_async_copy(
-            obuf.at[n % 2], o_hbm.at[1, :, pl.ds(n * TN, TN)], o_sem.at[n]
-        )
-
+    def put(n, i):
+        rows, cols = pl.ds(i * (T // 2), T // 2), pl.ds(n * CN, CN)
+        return pltpu.make_async_copy(obuf.at[rows, cols], o_hbm.at[1, rows, cols], o_sem.at[n, i])
+
+    get_st = pltpu.make_async_copy(st_hbm, st, s_sem)
+    get_st.start()
     for n in range(4):
-        get_q(n).start()
-    for n in range(4):
+        for g in range(2):
+            get_q(n, g).start()
+    get_first = pltpu.make_async_copy(first_hbm, fbuf, f_sem.at[0])
+    put_first = pltpu.make_async_copy(fbuf, o_hbm.at[0], f_sem.at[1])
+    cols_of[...] = jnp.zeros_like(cols_of)
+    rhs[...] = jnp.zeros_like(rhs)
+    get_st.wait()
+
+    def step(n, _):
+        for g in range(2):
+            get_q(n, g).wait()
         get_w(n).start()
-    get_first = pltpu.make_async_copy(first_hbm, fbuf, f_sem.at[0])
+        look_up(fq, st, rhs, cols_of, mixed, (n, n))
+        return 0
+
+    lax.fori_loop(0, 4, step, 0)
     get_first.start()
-    put_first = pltpu.make_async_copy(fbuf, o_hbm.at[0], f_sem.at[1])
-    look_up_columns(st_ref, rhs, cols_of)
-    for n in range(4):
-        get_q(n).wait()
-    look_up(fq, rhs, mixed, 0, H)
-    for n in range(4):
-        get_w(n).wait()
-        if n == 0:
+    for n in range(2):
+        get_w(2 * n).wait()
+        get_w(2 * n + 1).wait()
+        if n == 1:
             get_first.wait()
             put_first.start()
-        if n >= 2:
-            put(n - 2).wait()
-        cols = slice(n * TN, (n + 1) * TN)
-        obuf[n % 2] = jnp.dot(mixed[...], wbuf[:, cols], preferred_element_type=F32).astype(BF16)
-        put(n).start()
+        cols = slice(n * CN, (n + 1) * CN)
+        for i in range(2):
+            rows = slice(i * (T // 2), (i + 1) * (T // 2))
+            obuf[rows, cols] = jnp.dot(
+                mixed[rows, :], wbuf[:, cols], preferred_element_type=F32
+            ).astype(BF16)
+            put(n, i).start()
     put_first.wait()
-    put(2).wait()
-    put(3).wait()
+    for n in range(2):
+        for i in range(2):
+            put(n, i).wait()
 
 
 def finish(fq1, st1, w, out0):
@@ -499,18 +523,19 @@
     hbm = pl.BlockSpec(memory_space=pl.ANY)
     return pl.pallas_call(
         finish_kernel,
-        in_specs=[hbm, pl.BlockSpec(memory_space=pltpu.VMEM), hbm, hbm],
+        in_specs=[hbm] * 4,
         out_specs=hbm,
         out_shape=jax.ShapeDtypeStruct((B, T, 2048), BF16),
         scratch_shapes=[
             pltpu.VMEM((H, T, D), BF16),
-            pltpu.VMEM((H, 256, 256), BF16),
+            pltpu.VMEM((2, 4, ROWS, D), BF16),
+            pltpu.VMEM((4, 256, 256), BF16),
             pltpu.VMEM((D, D), F32),
             pltpu.VMEM((T, 2048), BF16),
             pltpu.VMEM((2048, 2048), BF16),
             pltpu.VMEM((T, 2048), BF16),
-            pltpu.VMEM((2, T, TN), BF16),
-            dma((4,)), dma((4,)), dma((2,)), dma((4,)),
+            pltpu.VMEM((T, 2048), BF16),
+            dma((4, 2)), dma, dma((4,)), dma((2,)), dma((2, 2)),
         ],
         compiler_params=pltpu.CompilerParams(vmem_limit_bytes=60 * 2**20),
         name="finish",

time: 69.8 us -> 65 us (0.931)
  Pallas kernels: 69.5 us -> 64.5 us
    pallas_call x1, Pallas kernels: 18.7 us -> 16 us  [finish(): pl.pallas_call(finish_kernel, in_specs=[hbm] * 4, out_specs=hbm, out_shap...]
    pallas_call x1, Pallas kernels: 50.8 us -> 48.5 us  [gather(): pl.pallas_call(gather_kernel, out_shape=(jax.ShapeDtypeStruct((2048, 2048...]
where the time goes in v3:
time: 65 us; the launch traced here: 64.7 us
  Pallas kernels  64.5 us (99%)
    pallas_call x1, Pallas kernels, gather(): pl.pallas_call(gather_kernel, out_shape=(jax.ShapeDtypeStruct((2048, 2048...  48.5 us
    pallas_call x1, Pallas kernels, finish(): pl.pallas_call(finish_kernel, in_specs=[hbm] * 4, out_specs=hbm, out_shap...  16 us

profile of v3, /device:TPU:0, one launch (start us, length us, event | category | flops | bytes accessed | tf_op | source)
XLA Modules:
  0.0 64.7 jit_solution(9169455490320828308)
XLA Ops:
  0.0 48.5 %gather.1 = (bf16[2048,2048]{1,0:T(8,128)(2,1)}, bf16[1024,2048]{1,0:T(8,128)(2,1)}, bf16[16,1024,128]{2,1,0:T(8,128)(2,1)}, bf16[2,4,272,128]{3,2,1,0:T(8,128)(2,1)}) custom-call(bf16[2,1024,16,128]{3,2,1,0:T(8,128)(2,1)} %q_hbm.1, bf16[2,1024,16,128]{3,2,1,0:T(8,128)(2,1)} %k_hbm.1, bf16[2,1024,16,128]{3,2,1,0:T(8,128)(2,1)} %v_hbm.1, bf16[256,2048]{1,0:T(8,128)(2,1)} %w_hbm.1), custom_call_target="tpu_custom_call" | custom-call | tf_op jit(solution)/shard_map/gather/pallas_call | solution.py:425
  48.5 16.0 %finish.1 = bf16[2,1024,2048]{2,1,0:T(8,128)(2,1)} custom-call(bf16[16,1024,128]{2,1,0:T(8,128)(2,1)} %get-tuple-element.9.fq_hbm, bf16[2,4,272,128]{3,2,1,0:T(8,128)(2,1)} %get-tuple-element.10.st_hbm, bf16[2048,2048]{1,0:T(8,128)(2,1)} %get-tuple-element.11.w_hbm, bf16[1024,2048]{1,0:T(8,128)(2,1)} %get-tuple-element.12.first_hbm), custom_call_target="tpu_custom_call" | custom-call | tf_op jit(solution)/shard_map/finish/pallas_call | solution.py:524
